TPU v7x, 32 devices: a whole 2x2x4 slice. The times are simulated.
32 devices in a mesh: dp: 4 (over y, x), expert: 8 (over z, core).
Axes of the slice: x: 2, y: 2, z: 4, core: 2. Of those that a mesh axis runs over, the one named last changes fastest.
Arguments:
- grad_out: bfloat16 [4096, 3072], P(('dp', 'expert')), may hold values from -6 to 6
- expert_ids: int32 [4096, 2], P(('dp', 'expert')), may hold values from 0 to 7, all different within a row; in each aligned block of 128 rows (0 to 127, 128 to 255, ...) at most 36 rows name the same one
- down_weight: bfloat16 [8, 1024, 3072], P('expert'), may hold values from -0.109375 to 0.109375
- history_grad: float32 [8, 8], replicated, may hold values from 0.5 to 3
- history_hidden: float32 [8, 8], replicated, may hold values from 0.5 to 3
Outputs:
- hidden_scaled: bfloat16 [4, 8, 288, 1024], P('dp', 'expert')
- new_history_grad: float32 [8, 8], replicated
- new_history_hidden: float32 [8, 8], replicated
Inputs may be any that keep to these rules, and one draw needn't show every extreme that they name: `expert_ids`: each row names 2 different experts; among the 128 rows of one device no expert is named more than 36 times, a bound that some block reaches in some devices.
All inputs are finite; a program needn't handle non-finite values.
Results may differ from a plain program's by a relative error of at most 0.0045.
Values may be sent and summed in bfloat16 or wider, within the bound.
No kernel may reach another device: no remote copies, remote signals or barrier semaphores. Data moves between devices by JAX's collectives and lax.ppermute only.
A program may use at most 128 MiB of HBM per device.

v0:
```python
import jax
import jax.numpy as jnp
from jax import lax
from jax.sharding import PartitionSpec as P


def per_device(grad_out, expert_ids, down_weight, history_grad, history_hidden):
    tok_rows = grad_out.shape[0]
    experts = history_grad.shape[1]
    slices = lax.axis_size("expert") // experts
    capacity = tok_rows * 9 // 32
    flat_ids = expert_ids.reshape(-1)
    onehot = (flat_ids[:, None] == jnp.arange(experts, dtype=jnp.int32)[None, :]).astype(jnp.int32)
    before = jnp.cumsum(onehot, axis=0) - onehot
    slot_index = jnp.sum(before * onehot, axis=1)
    target = flat_ids * capacity + slot_index
    matches = (jnp.arange(experts * capacity, dtype=jnp.int32)[:, None] == target[None, :]).astype(
        jnp.int32
    )
    dispatch = jnp.sum(matches.reshape(experts * capacity, tok_rows, 2), axis=2).astype(
        jnp.bfloat16
    )
    gathered = jnp.dot(dispatch, grad_out, preferred_element_type=jnp.float32)
    scale_in = 1.0 / jnp.max(history_grad, axis=0)
    scale_hidden = 1.0 / jnp.max(history_hidden, axis=0)
    quantized = jnp.clip(
        gathered.reshape(experts, capacity, -1) * scale_in[:, None, None], -1.0, 1.0
    ).astype(jnp.bfloat16)
    own_index = lax.axis_index("expert")
    own_expert = own_index // slices
    chosen = jnp.arange(experts, dtype=jnp.int32) == own_expert
    own_scale_in = jnp.sum(jnp.where(chosen, scale_in, 0.0))
    own_scale_hidden = jnp.sum(jnp.where(chosen, scale_hidden, 0.0))
    routed = jnp.max(onehot.reshape(tok_rows, 2, experts), axis=1) > 0
    row_peak = jnp.max(jnp.abs(grad_out.astype(jnp.float32)), axis=1)
    grad_peak = jnp.max(jnp.where(routed, row_peak[:, None], 0.0), axis=0)
    weight_block = down_weight[0]
    outgoing = jnp.repeat(quantized, slices, axis=0)
    received = lax.all_to_all(outgoing, "expert", split_axis=0, concat_axis=0, tiled=True)
    product = jnp.einsum("sic,uc->siu", received, weight_block, preferred_element_type=jnp.float32)
    hidden = product / own_scale_in
    hidden_peak = jnp.max(jnp.abs(hidden))
    hidden_vec = jnp.where(chosen, hidden_peak, 0.0)
    grad_amax, hidden_amax = lax.pmax((grad_peak, hidden_vec), ("dp", "expert"))
    scaled = jnp.clip(hidden * own_scale_hidden, -1.0, 1.0).astype(jnp.bfloat16)
    hidden_scaled = scaled.reshape(1, 1, -1, scaled.shape[2])
    new_history_grad = jnp.concatenate([history_grad[1:], grad_amax[None, :]], axis=0)
    new_history_hidden = jnp.concatenate([history_hidden[1:], hidden_amax[None, :]], axis=0)
    return (hidden_scaled, new_history_grad, new_history_hidden)


def solution(mesh):
    in_specs = (
        P(("dp", "expert"), None),
        P(("dp", "expert"), None),
        P("expert", None, None),
        P(),
        P(),
    )
    out_specs = (P("dp", "expert", None, None), P(), P())
    return jax.shard_map(
        per_device, mesh=mesh, in_specs=in_specs, out_specs=out_specs, check_vma=False
    )
```

profile of v0, /device:TPU:0, one launch (start us, length us, event | category | flops | bytes accessed | tf_op | source)
XLA Modules:
  0.0 111.7 jit_solution(3754334476926324953)
XLA Ops:
  0.6 0.8 copy.20
  1.4 0.1 eq.57
  1.6 0.1 eq.53
  1.7 0.6 reduce-window.6
  2.3 0.2 slice_reduce_fusion
  2.6 0.1 fusion.8
  2.7 0.1 reduce_sum.39
  2.8 0.1 copy.22
  2.9 0.7 multiply_add_fusion
  3.6 1.7 %fusion.5 = f32[288,3072]{1,0:T(8,128)S(1)} fusion(bf16[128,3072]{1,0:T(8,128)(2,1)} %param.5, s32[288,128]{1,0:T(8,128)S(1)} %convert_reduce_fusion), kind=kOutput, calls=%fused_computation.9 | convolution fusion | flops 226529280 | bytes 4472832 | tf_op jit(solution)/shard_map/dot_general | solution.py:23
  5.4 0.0 copy-start.1
  5.4 2.1 %reshape.61 = f32[8,36,3072]{2,1,0:T(8,128)} reshape(f32[288,3072]{1,0:T(8,128)S(1)} %fusion.5) | data formatting | bytes 7077888 | tf_op jit(solution)/shard_map/reshape | solution.py:27
  7.5 0.6 select_reduce_fusion.1
  8.1 3.8 %clamp_convert_fusion = bf16[8,36,3072]{2,1,0:T(8,128)(2,1)} fusion(f32[8,36,3072]{2,1,0:T(8,128)} %reshape.61, f32[8]{0:T(128)S(1)} %get-tuple-element.6), kind=kLoop, calls=%fused_computation.2 | loop fusion | flops 2654208 | bytes 5308448 | tf_op jit(solution)/shard_map/convert_element_type | solution.py:28
  11.9 6.5 %all-to-all-start = ((bf16[8,36,3072]{2,1,0:T(8,128)(2,1)}), bf16[8,36,3072]{2,1,0:T(8,128)(2,1)S(1)}, u32[]{:S(2)}, u32[]{:S(2)}) async-start(bf16[8,36,3072]{2,1,0:T(8,128)(2,1)} %clamp_convert_fusion), calls=%async_computation | async-start | bytes 3932160 | tf_op jit(solution)/shard_map/all_to_all | solution.py:39
  18.5 0.2 abs_reduce_fusion
  18.7 0.1 select_reduce_fusion
  18.8 0.6 fusion.10
  19.4 45.2 %all-to-all-done = bf16[8,36,3072]{2,1,0:T(8,128)(2,1)S(1)} async-done(((bf16[8,36,3072]{2,1,0:T(8,128)(2,1)}), bf16[8,36,3072]{2,1,0:T(8,128)(2,1)S(1)}, u32[]{:S(2)}, u32[]{:S(2)}) %all-to-all-start) | async-done | bytes 1769504 | tf_op jit(solution)/shard_map/all_to_all | solution.py:39
  64.6 7.1 %abs_reduce_fusion.1 = (f32[]{:T(128)}, bf16[8,36,1024]{2,1,0:T(8,128)(2,1)S(1)}) fusion(f32[]{:T(128)} %fusion.10, f32[]{:T(128)} %get-tuple-element.5, bf16[8,36,3072]{2,1,0:T(8,128)(2,1)S(1)} %all-to-all-done, bf16[1,1024,3072]{2,1,0:T(8,128)(2,1)} %param.7), kind=kOutput, calls=%fused_computation.4 | convolution fusion | flops 1813708800 | bytes 8650764 | tf_op jit(solution)/shard_map/sic,uc->siu/dot_general | solution.py:40
  71.7 0.6 select_bitcast_fusion
  72.4 0.9 reshape.62
  73.3 37.8 %all-reduce = (f32[1,8]{1,0:T(1,128)S(1)}, f32[1,8]{1,0:T(1,128)S(1)}) all-reduce(f32[1,8]{1,0:T(1,128)S(1)} %bitcast.21, f32[1,8]{1,0:T(1,128)S(1)} %select_bitcast_fusion), channel_id=1, replica_groups=mesh['dp'=4,'expert'=8] {'dp','expert'}, use_global_device_ids=true, to_apply=%region_11.12 | all-reduce | flops 16 | bytes 128 | tf_op jit(solution)/shard_map/pmax | solution.py:44
  111.1 0.6 pad_maximum_fusion
  (16 shorter events, 0.1 us)
Async XLA Ops:
  5.4 2.1 %copy-start.1 = (f32[8,8]{1,0:T(8,128)S(1)}, f32[8,8]{1,0:T(8,128)}, u32[]{:S(2)}) copy-start(f32[8,8]{1,0:T(8,128)} %param.8) | copy-start | bytes 772
  11.9 6.5 %copy-start.2 = (f32[8,8]{1,0:T(8,128)S(1)}, f32[8,8]{1,0:T(8,128)}, u32[]{:S(2)}) copy-start(f32[8,8]{1,0:T(8,128)} %param.9) | copy-start | bytes 772
  11.9 6.5 %copy-start.3 = (s32[128,2]{0,1:T(2,128)S(1)}, s32[128,2]{0,1:T(2,128)}, u32[]{:S(2)}) copy-start(s32[128,2]{0,1:T(2,128)} %param.6) | copy-start | bytes 3076
  11.9 6.6 %copy-start = (bf16[128,3072]{1,0:T(8,128)(2,1)S(1)}, bf16[128,3072]{1,0:T(8,128)(2,1)}, u32[]{:S(2)}) copy-start(bf16[128,3072]{1,0:T(8,128)(2,1)} %param.5) | copy-start | bytes 2359300
  11.9 52.7 %all-to-all-start = ((bf16[8,36,3072]{2,1,0:T(8,128)(2,1)}), bf16[8,36,3072]{2,1,0:T(8,128)(2,1)S(1)}, u32[]{:S(2)}, u32[]{:S(2)}) async-start(bf16[8,36,3072]{2,1,0:T(8,128)(2,1)} %clamp_convert_fusion), calls=%async_computation | async-start | bytes 3932160 | tf_op jit(solution)/shard_map/all_to_all | solution.py:39
where the time goes:
time: 113 us; the launch traced here: 112 us
  waiting for transfers between devices  45.2 us (40%)
  blocking collectives  37.8 us (33%)
  matrix products  8.85 us (8%)
  other arithmetic  8.16 us (7%)
  starting transfers between devices  6.49 us (6%)
  local copies, waits for them, and re-layouts  4.51 us (4%)
    all_to_all x1, waiting for transfers between devices, per_device(): lax.all_to_all(outgoing, 'expert', split_axis=0, concat_axis=0, tiled=True)  45.2 us
    pmax x1, blocking collectives, per_device(): grad_amax, hidden_amax = lax.pmax((grad_peak, hidden_vec), ('dp', 'expert'))  37.8 us
    dot_general x1, matrix products, per_device(): jnp.einsum('sic,uc->siu', received, weight_block, preferred_element_type=...  7.11 us
    all_to_all x1, starting transfers between devices, per_device(): lax.all_to_all(outgoing, 'expert', split_axis=0, concat_axis=0, tiled=True)  6.49 us
    convert_element_type x1, other arithmetic, per_device(): quantized = jnp.clip(gathered.reshape(experts, capacity, -1) * scale_in[:...  3.85 us
  transfers between devices with their start and end apart: 1, of which 1 were waited for; matrix products, arithmetic and copies ran while one was open for 1% of the time, Pallas kernels for 0%

commit v1 on v0

--- a/solution.py
+++ b/solution.py
@@ -1,10 +1,221 @@
+import functools
+
 import jax
 import jax.numpy as jnp
 from jax import lax
+from jax.experimental import pallas as pl
+from jax.experimental.pallas import tpu as pltpu
 from jax.sharding import PartitionSpec as P
 
-
-def per_device(grad_out, expert_ids, down_weight, history_grad, history_hidden):
+VMEM = pl.BlockSpec(memory_space=pltpu.VMEM)
+
+
+def choice_map(ids, order, experts):
+    return (ids[0:1, :] == order) | (ids[1:2, :] == order)
+
+
+def pick(values, index):
+    lanes = lax.broadcasted_iota(jnp.int32, values.shape, 1)
+    return jnp.sum(jnp.where(lanes == index, values, 0.0), axis=1, keepdims=True)
+
+
+def dispatch_kernel(experts, capacity, ids_ref, grad_ref, history_ref, *out_refs):
+    tokens, features = grad_ref.shape
+    half = features // 2
+    me = lax.axis_index("expert")
+    ids = ids_ref[...]
+    order = lax.broadcasted_iota(jnp.int32, (experts, tokens), 0) ^ me
+    named = choice_map(ids, order, experts)
+    before = (
+        lax.broadcasted_iota(jnp.int32, (tokens, tokens), 0)
+        < lax.broadcasted_iota(jnp.int32, (tokens, tokens), 1)
+    )
+    slot = jnp.dot(
+        jnp.where(named, 1.0, 0.0).astype(jnp.bfloat16),
+        jnp.where(before, 1.0, 0.0).astype(jnp.bfloat16),
+        preferred_element_type=jnp.float32,
+    ).astype(jnp.int32)
+    slot = jnp.where(named, slot, -1 - 2 * capacity)
+    scale = 1.0 / jnp.max(history_ref[...], axis=0, keepdims=True)
+    rows = lax.broadcasted_iota(jnp.int32, (2 * capacity, tokens), 0)
+    stacked = jnp.concatenate([grad_ref[:, :half], grad_ref[:, half:]], axis=0)
+    for k in range(experts):
+        mine = slot[k : k + 1, :]
+        top = jnp.where(mine == rows, 1.0, 0.0)
+        bottom = jnp.where(mine == rows - capacity, 1.0, 0.0)
+        select = jnp.concatenate([top, bottom], axis=1).astype(jnp.bfloat16)
+        rowsum = jnp.dot(select, stacked, preferred_element_type=jnp.float32)
+        factor = pick(scale, me ^ k)
+        out_refs[k][...] = jnp.clip(rowsum * factor, -1.0, 1.0).astype(jnp.bfloat16)
+
+
+def project(blocks, capacity, weight_ref, history_grad_ref, history_hidden_ref, low_ref, high_ref, pair_refs):
+    me = lax.axis_index("expert")
+    part = blocks[0].shape[0] // 2 + 4
+    offset = 2 * capacity - part
+    half = weight_ref.shape[1] // 2
+    for i, block in enumerate(blocks):
+        low_ref[i * part : (i + 1) * part, :] = block[0:part, :]
+        high_ref[i * part : (i + 1) * part, :] = block[offset:, :]
+    contract = (((1,), (1,)), ((), ()))
+    low = lax.dot_general(
+        low_ref[...], weight_ref[:, :half], contract, preferred_element_type=jnp.float32
+    )
+    high = lax.dot_general(
+        high_ref[...], weight_ref[:, half:], contract, preferred_element_type=jnp.float32
+    )
+    skip = capacity - offset
+    products = [
+        low[i * part : i * part + capacity] + high[i * part + skip : i * part + skip + capacity]
+        for i in range(len(blocks))
+    ]
+    scale_in = pick(1.0 / jnp.max(history_grad_ref[...], axis=0, keepdims=True), me)
+    scale_hidden = pick(1.0 / jnp.max(history_hidden_ref[...], axis=0, keepdims=True), me)
+    restore = 1.0 / scale_in
+    peak = functools.reduce(jnp.maximum, [jnp.abs(p) for p in products])
+    peak = jnp.max(jnp.max(peak, axis=0, keepdims=True), axis=1, keepdims=True) * restore
+    first_core = (me & 1) == 0
+    for j, ref in enumerate(pair_refs):
+        a = jnp.clip(products[2 * j] * restore * scale_hidden, -1.0, 1.0)
+        b = jnp.clip(products[2 * j + 1] * restore * scale_hidden, -1.0, 1.0)
+        top, bottom = jnp.where(first_core, a, b), jnp.where(first_core, b, a)
+        ref[...] = jnp.concatenate([top, bottom], axis=0).astype(jnp.bfloat16)
+    return peak
+
+
+def early_kernel(experts, capacity, count, *refs):
+    blocks = refs[:count]
+    weight_ref, history_grad_ref, history_hidden_ref, ids_ref, grad_ref = refs[count : count + 5]
+    outs = refs[count + 5 : -2]
+    low_ref, high_ref = refs[-2:]
+    me = lax.axis_index("expert")
+    peak = project(
+        blocks, capacity, weight_ref, history_grad_ref, history_hidden_ref, low_ref, high_ref, outs[:-1]
+    )
+    tokens = grad_ref.shape[0]
+    order = lax.broadcasted_iota(jnp.int32, (experts, tokens), 0)
+    named = choice_map(ids_ref[...], order, experts)
+    row_peak = jnp.max(jnp.abs(grad_ref[...].astype(jnp.float32)), axis=1, keepdims=True)
+    row_peak = jnp.broadcast_to(row_peak, (tokens, tokens)).T[0:1, :]
+    grad_peak = jnp.max(jnp.where(named, row_peak, 0.0), axis=1, keepdims=True)
+    lanes = lax.broadcasted_iota(jnp.int32, (experts, 128), 1)
+    spread = jnp.where(
+        lanes == lax.broadcasted_iota(jnp.int32, (experts, 128), 0), grad_peak, 0.0
+    )
+    vector = jnp.max(spread, axis=0, keepdims=True)
+    lane = lax.broadcasted_iota(jnp.int32, (1, 128), 1)
+    outs[-1][...] = jnp.where(lane == experts + me, peak, vector)
+
+
+def late_kernel(experts, capacity, count, *refs):
+    blocks = refs[:count]
+    weight_ref, history_grad_ref, history_hidden_ref, vector_ref = refs[count : count + 4]
+    outs = refs[count + 4 : -2]
+    low_ref, high_ref = refs[-2:]
+    me = lax.axis_index("expert")
+    peak = project(
+        blocks, capacity, weight_ref, history_grad_ref, history_hidden_ref, low_ref, high_ref, outs[:-1]
+    )
+    lane = lax.broadcasted_iota(jnp.int32, (1, 128), 1)
+    vector = jnp.maximum(vector_ref[...], jnp.where(lane == experts + me, peak, 0.0))
+    outs[-1][...] = jnp.broadcast_to(vector, outs[-1].shape)
+
+
+def assemble_kernel(capacity, *refs):
+    pairs, out_ref = refs[:-1], refs[-1]
+    chip = lax.axis_index("expert") // 2
+    for j, ref in enumerate(pairs):
+        start = pl.multiple_of((chip ^ j) * 2 * capacity, 8)
+        out_ref[pl.ds(start, 2 * capacity), :] = ref[...]
+
+
+def finish_kernel(experts, peaks_ref, history_grad_ref, history_hidden_ref, grad_out_ref, hidden_out_ref):
+    peaks = jnp.max(peaks_ref[...], axis=0, keepdims=True)
+    history = history_grad_ref.shape[0]
+    for ref, out, at in (
+        (history_grad_ref, grad_out_ref, 0),
+        (history_hidden_ref, hidden_out_ref, experts),
+    ):
+        out[0 : history - 1, :] = ref[1:history, :]
+        out[history - 1 : history, :] = peaks[:, at : at + experts]
+
+
+def fast_device(grad_out, expert_ids, down_weight, history_grad, history_hidden):
+    tokens, features = grad_out.shape
+    experts = history_grad.shape[1]
+    capacity = tokens * 9 // 32
+    units = down_weight.shape[1]
+    half = experts // 2
+    devices = lax.axis_size("dp") * lax.axis_size("expert")
+    ids = expert_ids.T
+    weight = down_weight[0]
+    bf16, f32 = jnp.bfloat16, jnp.float32
+    block = jax.ShapeDtypeStruct((2 * capacity, features // 2), bf16)
+    outgoing = pl.pallas_call(
+        functools.partial(dispatch_kernel, experts, capacity),
+        out_shape=[block] * experts,
+        in_specs=[VMEM] * 3,
+        out_specs=[VMEM] * experts,
+        compiler_params=pltpu.CompilerParams(vmem_limit_bytes=16 << 20),
+        name="dispatch",
+    )(ids, grad_out, history_grad)
+    order = list(range(2, half)) + list(range(half, experts)) + [1]
+    received = [outgoing[0]] + [None] * (experts - 1)
+    for k in order:
+        received[k] = lax.ppermute(
+            outgoing[k], "expert", [(i, i ^ k) for i in range(experts)]
+        )
+    pair = jax.ShapeDtypeStruct((2 * capacity, units), bf16)
+    scratch = [pltpu.VMEM((half * (capacity + 4), features // 2), bf16)] * 2
+    params = pltpu.CompilerParams(vmem_limit_bytes=24 << 20)
+    cost = pl.CostEstimate(
+        flops=half * capacity * units * features * 2,
+        bytes_accessed=units * features * 2,
+        transcendentals=0,
+    )
+    *early, vector = pl.pallas_call(
+        functools.partial(early_kernel, experts, capacity, half),
+        out_shape=[pair] * (half // 2) + [jax.ShapeDtypeStruct((1, 128), f32)],
+        in_specs=[VMEM] * (half + 5),
+        out_specs=[VMEM] * (half // 2 + 1),
+        scratch_shapes=scratch,
+        compiler_params=params,
+        cost_estimate=cost,
+        name="early",
+    )(*received[:half], weight, history_grad, history_hidden, ids, grad_out)
+    *late, peaks = pl.pallas_call(
+        functools.partial(late_kernel, experts, capacity, half),
+        out_shape=[pair] * (half // 2) + [jax.ShapeDtypeStruct((devices, 128), f32)],
+        in_specs=[VMEM] * (half + 4),
+        out_specs=[VMEM] * (half // 2 + 1),
+        scratch_shapes=scratch,
+        compiler_params=params,
+        cost_estimate=cost,
+        name="late",
+    )(*received[half:], weight, history_grad, history_hidden, vector)
+    everyone = lax.all_to_all(peaks, ("dp", "expert"), 0, 0, tiled=True)
+    hidden = pl.pallas_call(
+        functools.partial(assemble_kernel, capacity),
+        out_shape=jax.ShapeDtypeStruct((experts * capacity, units), bf16),
+        in_specs=[VMEM] * half,
+        out_specs=VMEM,
+        compiler_params=pltpu.CompilerParams(vmem_limit_bytes=8 << 20),
+        cost_estimate=pl.CostEstimate(
+            flops=1 << 22, bytes_accessed=experts * capacity * units * 4, transcendentals=0
+        ),
+        name="assemble",
+    )(*early, *late)
+    new_history_grad, new_history_hidden = pl.pallas_call(
+        functools.partial(finish_kernel, experts),
+        out_shape=[jax.ShapeDtypeStruct(history_grad.shape, f32)] * 2,
+        in_specs=[VMEM] * 3,
+        out_specs=[VMEM] * 2,
+        name="finish",
+    )(everyone, history_grad, history_hidden)
+    return hidden.reshape(1, 1, -1, units), new_history_grad, new_history_hidden
+
+
+def general_device(grad_out, expert_ids, down_weight, history_grad, history_hidden):
     tok_rows = grad_out.shape[0]
     experts = history_grad.shape[1]
     slices = lax.axis_size("expert") // experts
@@ -49,6 +260,14 @@
     return (hidden_scaled, new_history_grad, new_history_hidden)
 
 
+def per_device(grad_out, expert_ids, down_weight, history_grad, history_hidden):
+    experts = history_grad.shape[1]
+    whole_experts = lax.axis_size("expert") == experts
+    paired = experts & (experts - 1) == 0 and experts >= 4
+    device = fast_device if whole_experts and paired else general_device
+    return device(grad_out, expert_ids, down_weight, history_grad, history_hidden)
+
+
 def solution(mesh):
     in_specs = (
         P(("dp", "expert"), None),

time: 113 us -> 66.7 us (0.59)
  blocking collectives: 37.8 us -> 0 us
  waiting for transfers between devices: 45.2 us -> 22.3 us
  starting transfers between devices: 6.49 us -> 24.9 us
  Pallas kernels: 0 us -> 9.31 us
  matrix products: 8.85 us -> 0 us
  other arithmetic: 8.16 us -> 0 us
  local copies, waits for them, and re-layouts: 4.51 us -> 9.06 us
    all_to_all x1, waiting for transfers between devices: 45.2 us -> 6.29 us  [fast_device(): everyone = lax.all_to_all(peaks, ('dp', 'expert'), 0, 0, tiled=True)]
    pmax x1 -> x0, blocking collectives: 37.8 us -> none  [per_device(): grad_amax, hidden_amax = lax.pmax((grad_peak, hidden_vec), ('dp', 'expert'))]
    ppermute x0 -> x7, waiting for transfers between devices: none -> 16 us  [fast_device(): lax.ppermute(outgoing[k], 'expert', [(i, i ^ k) for i in range(experts)])]
    ppermute x0 -> x7, starting transfers between devices: none -> 10 us  [fast_device(): lax.ppermute(outgoing[k], 'expert', [(i, i ^ k) for i in range(experts)])]
    pallas_call x0 -> x5, Pallas kernels: none -> 9.31 us  [the longest x1 3.06 us: fast_device(): pl.pallas_call(functools.partial(late_kernel, experts, capacity, half), o...]
    dot_general x2 -> x0, matrix products: 8.85 us -> none  [the longest x1 7.11 us: per_device(): jnp.einsum('sic,uc->siu', received, weight_block, preferred_element_type=...]
    all_to_all x1, starting transfers between devices: 6.49 us -> 14.9 us  [fast_device(): everyone = lax.all_to_all(peaks, ('dp', 'expert'), 0, 0, tiled=True)]
    unnamed x9 -> x20, local copies, waits for them, and re-layouts: 0.8 us -> 9.06 us
  transfers between devices with their start and end apart: 1 -> 8, of which waited for: 1 -> 4; matrix products, arithmetic and copies ran while one was open for 1% -> 0% of each run, Pallas kernels for 0% -> 5%
where the time goes in v1:
time: 66.7 us; the launch traced here: 66.3 us
  starting transfers between devices  24.9 us (37%)
  waiting for transfers between devices  22.3 us (33%)
  Pallas kernels  9.31 us (14%)
  local copies, waits for them, and re-layouts  9.06 us (14%)
  between operations  0.69 us (1%)
    ppermute x7, waiting for transfers between devices, fast_device(): lax.ppermute(outgoing[k], 'expert', [(i, i ^ k) for i in range(experts)])  16 us
    all_to_all x1, starting transfers between devices, fast_device(): everyone = lax.all_to_all(peaks, ('dp', 'expert'), 0, 0, tiled=True)  14.9 us
    ppermute x7, starting transfers between devices, fast_device(): lax.ppermute(outgoing[k], 'expert', [(i, i ^ k) for i in range(experts)])  10 us
    unnamed x20, local copies, waits for them, and re-layouts  9.06 us
    all_to_all x1, waiting for transfers between devices, fast_device(): everyone = lax.all_to_all(peaks, ('dp', 'expert'), 0, 0, tiled=True)  6.29 us
    pallas_call x1, Pallas kernels, fast_device(): pl.pallas_call(functools.partial(late_kernel, experts, capacity, half), o...  3.06 us
    pallas_call x1, Pallas kernels, fast_device(): pl.pallas_call(functools.partial(early_kernel, experts, capacity, half),...  2.64 us
    pallas_call x1, Pallas kernels, fast_device(): pl.pallas_call(functools.partial(finish_kernel, experts), out_shape=[jax....  1.41 us
  transfers between devices with their start and end apart: 8, of which 4 were waited for; matrix products, arithmetic and copies ran while one was open for 0% of the time, Pallas kernels for 5%

profile of v1, /device:TPU:0, one launch (start us, length us, event | category | flops | bytes accessed | tf_op | source)
XLA Modules:
  0.0 66.3 jit_solution(2858639404321685214)
XLA Ops:
  0.6 1.1 %copy-done.2 = bf16[128,3072]{1,0:T(8,128)(2,1)S(1)} copy-done((bf16[128,3072]{1,0:T(8,128)(2,1)S(1)}, bf16[128,3072]{1,0:T(8,128)(2,1)}, u32[]{:S(2)}) %copy-start.2) | copy-done | bytes 786456
  1.8 0.7 %copy-done.4 = f32[8,8]{1,0:T(8,128)S(1)} copy-done((f32[8,8]{1,0:T(8,128)S(1)}, f32[8,8]{1,0:T(8,128)}, u32[]{:S(2)}) %copy-start.4) | copy-done | bytes 280
  2.5 0.7 %copy-done.7 = s32[128,2]{0,1:T(2,128)S(1)} copy-done((s32[128,2]{0,1:T(2,128)S(1)}, s32[128,2]{0,1:T(2,128)}, u32[]{:S(2)}) %copy-start.7) | copy-done | bytes 1048
  3.1 1.3 %dispatch.1 = (bf16[72,1536]{1,0:T(8,128)(2,1)S(1)}, bf16[72,1536]{1,0:T(8,128)(2,1)S(1)}, bf16[72,1536]{1,0:T(8,128)(2,1)S(1)}, bf16[72,1536]{1,0:T(8,128)(2,1)...) custom-call(s32[2,128]{1,0:T(2,128)S(1)} %bitcast.9, ...), custom_call_target="tpu_custom_call" | custom-call | tf_op jit(solution)/shard_map/dispatch/pallas_call | solution.py:154
  4.5 0.6 collective-permute-start
  5.0 2.6 %collective-permute-start.1 = (bf16[72,1536]{1,0:T(8,128)(2,1)S(1)}, bf16[72,1536]{1,0:T(8,128)(2,1)S(1)}, u32[]{:S(2)}, u32[]{:S(2)}) collective-permute-start(bf16[72,1536]{1,0:T(8,128)(2,1)S(1)} %get-tuple-element.21), channel_id=1, source_target_pairs={{0,2},{1,3},{2,0},{3,1},{4,6},{5,7},{6,4},{7,5},{8,10},{9,11},{10,... | collective-permute-start | bytes 663560 | tf_op jit(solution)/shard_map/ppermute | solution.py:165
  7.7 2.8 %collective-permute-start.3 = (bf16[72,1536]{1,0:T(8,128)(2,1)S(1)}, bf16[72,1536]{1,0:T(8,128)(2,1)S(1)}, u32[]{:S(2)}, u32[]{:S(2)}) collective-permute-start(bf16[72,1536]{1,0:T(8,128)(2,1)S(1)} %get-tuple-element.25), channel_id=1, source_target_pairs={{0,4},{1,5},{2,6},{3,7},{4,0},{5,1},{6,2},{7,3},{8,12},{9,13},{10,... | collective-permute-start | bytes 663560 | tf_op jit(solution)/shard_map/ppermute | solution.py:165
  10.5 3.6 %collective-permute-start.5 = (bf16[72,1536]{1,0:T(8,128)(2,1)S(1)}, bf16[72,1536]{1,0:T(8,128)(2,1)S(1)}, u32[]{:S(2)}, u32[]{:S(2)}) collective-permute-start(bf16[72,1536]{1,0:T(8,128)(2,1)S(1)} %get-tuple-element.27), channel_id=1, source_target_pairs={{0,6},{1,7},{2,4},{3,5},{4,2},{5,3},{6,0},{7,1},{8,14},{9,15},{10,... | collective-permute-start | bytes 663560 | tf_op jit(solution)/shard_map/ppermute | solution.py:165
  14.1 8.8 %collective-permute-done.1.refs_2_ = bf16[72,1536]{1,0:T(8,128)(2,1)S(1)} collective-permute-done((bf16[72,1536]{1,0:T(8,128)(2,1)S(1)}, bf16[72,1536]{1,0:T(8,128)(2,1)S(1)}, u32[]{:S(2)}, u32[]{:S(2)}) %collective-permute-start.1) | collective-permute-done | bytes 221216 | tf_op jit(solution)/shard_map/ppermute | solution.py:165
  22.9 0.4 collective-permute-start.6
  23.3 3.8 %collective-permute-done.2.refs_3_ = bf16[72,1536]{1,0:T(8,128)(2,1)S(1)} collective-permute-done((bf16[72,1536]{1,0:T(8,128)(2,1)S(1)}, bf16[72,1536]{1,0:T(8,128)(2,1)S(1)}, u32[]{:S(2)}, u32[]{:S(2)}) %collective-permute-start.2) | collective-permute-done | bytes 221216 | tf_op jit(solution)/shard_map/ppermute | solution.py:165
  27.2 2.8 %copy-done = bf16[1,1024,3072]{2,1,0:T(8,128)(2,1)S(1)} copy-done((bf16[1,1024,3072]{2,1,0:T(8,128)(2,1)S(1)}, bf16[1,1024,3072]{2,1,0:T(8,128)(2,1)}, u32[]{:S(2)}) %copy-start) | copy-done | bytes 6291480
  29.9 1.1 %copy-done.3 = bf16[128,3072]{1,0:T(8,128)(2,1)S(1)} copy-done((bf16[128,3072]{1,0:T(8,128)(2,1)S(1)}, bf16[128,3072]{1,0:T(8,128)(2,1)}, u32[]{:S(2)}) %copy-start.3) | copy-done | bytes 786456
  31.1 0.7 %copy-done.5 = f32[8,8]{1,0:T(8,128)S(1)} copy-done((f32[8,8]{1,0:T(8,128)S(1)}, f32[8,8]{1,0:T(8,128)}, u32[]{:S(2)}) %copy-start.5) | copy-done | bytes 280
  31.8 0.7 %copy-done.6 = f32[8,8]{1,0:T(8,128)S(1)} copy-done((f32[8,8]{1,0:T(8,128)S(1)}, f32[8,8]{1,0:T(8,128)}, u32[]{:S(2)}) %copy-start.6) | copy-done | bytes 280
  32.4 0.7 %copy-done.8 = s32[128,2]{0,1:T(2,128)S(1)} copy-done((s32[128,2]{0,1:T(2,128)S(1)}, s32[128,2]{0,1:T(2,128)}, u32[]{:S(2)}) %copy-start.8) | copy-done | bytes 1048
  33.1 2.6 %early.1 = (bf16[72,1024]{1,0:T(8,128)(2,1)S(1)}, bf16[72,1024]{1,0:T(8,128)(2,1)S(1)}, f32[1,128]{1,0:T(1,128)S(1)}) custom-call(bf16[72,1536]{1,0:T(8,128)(2,1)S(1)} %get-tuple-element.19.refs_0_, bf16[72,1536]{1,0:T(8,128)(2,1)S(1)} %collective-permute-done.refs_1_, bf16[72,1536]{1,0:T(8,128)(2,1)S(1)} %collective-permute-done.1.refs_2_, ...), custom_call_target="tpu_custom_call" | custom-call | flops 905969664 | bytes 6291456 | tf_op jit(solution)/shard_map/early/pallas_call | solution.py:176
  35.8 3.3 %collective-permute-done.6.refs_3_ = bf16[72,1536]{1,0:T(8,128)(2,1)S(1)} collective-permute-done((bf16[72,1536]{1,0:T(8,128)(2,1)S(1)}, bf16[72,1536]{1,0:T(8,128)(2,1)S(1)}, u32[]{:S(2)}, u32[]{:S(2)}) %collective-permute-start.6) | collective-permute-done | bytes 221216 | tf_op jit(solution)/shard_map/ppermute | solution.py:165
  39.1 3.1 %late.1 = (bf16[72,1024]{1,0:T(8,128)(2,1)S(1)}, bf16[72,1024]{1,0:T(8,128)(2,1)S(1)}, f32[32,128]{1,0:T(8,128)}) custom-call(bf16[72,1536]{1,0:T(8,128)(2,1)S(1)} %collective-permute-done.3.refs_0_, bf16[72,1536]{1,0:T(8,128)(2,1)S(1)} %collective-permute-done.4.refs_1_, bf16[72,1536]{1,0:T(8,128)(2,1)S(1)} %collective-permute-done.5.refs_2_, ...), custom_call_target="tpu_custom_call" | custom-call | flops 905969664 | bytes 6291456 | tf_op jit(solution)/shard_map/late/pallas_call | solution.py:186
  42.2 14.9 %all-to-all-start = ((f32[32,1,128]{2,1,0:T(1,128)}), f32[32,1,128]{2,1,0:T(1,128)S(1)}, u32[]{:S(2)}, u32[]{:S(2)}) async-start(f32[32,1,128]{2,1,0:T(1,128)} %bitcast.4), calls=%async_computation | async-start | bytes 32768 | tf_op jit(solution)/shard_map/all_to_all | solution.py:196
  57.1 0.9 %assemble.1 = bf16[288,1024]{1,0:T(8,128)(2,1)} custom-call(bf16[72,1024]{1,0:T(8,128)(2,1)S(1)} %get-tuple-element.23.refs_0_, bf16[72,1024]{1,0:T(8,128)(2,1)S(1)} %get-tuple-element.24.refs_1_, bf16[72,1024]{1,0:T(8,128)(2,1)S(1)} %get-tuple-element.30.refs_2_, bf16[72,1024]{1,0:T(8,128)(2,1)S(1)} %get-tuple-element.31.refs_3_), custom_call_target="tpu_custom_call" | custom-call | flops 4194304 | bytes 1179648 | tf_op jit(solution)/shard_map/assemble/pallas_call | solution.py:197
  58.0 6.3 %all-to-all-done = f32[32,1,128]{2,1,0:T(1,128)S(1)} async-done(((f32[32,1,128]{2,1,0:T(1,128)}), f32[32,1,128]{2,1,0:T(1,128)S(1)}, u32[]{:S(2)}, u32[]{:S(2)}) %all-to-all-start) | async-done | bytes 16416 | tf_op jit(solution)/shard_map/all_to_all | solution.py:196
  64.3 0.6 copy-done.9
  64.9 1.4 %finish.1 = (f32[8,8]{1,0:T(8,128)}, f32[8,8]{1,0:T(8,128)}) custom-call(f32[32,128]{1,0:T(8,128)} %bitcast.12, f32[8,8]{1,0:T(8,128)} %history_grad_ref.1, f32[8,8]{1,0:T(8,128)} %history_hidden_ref.1), custom_call_target="tpu_custom_call" | custom-call | tf_op jit(solution)/shard_map/finish/pallas_call | solution.py:208
  (17 shorter events, 0.1 us)
Async XLA Ops:
  0.6 1.1 %copy-start.2 = (bf16[128,3072]{1,0:T(8,128)(2,1)S(1)}, bf16[128,3072]{1,0:T(8,128)(2,1)}, u32[]{:S(2)}) copy-start(bf16[128,3072]{1,0:T(8,128)(2,1)} %refs_8_.1) | copy-start | bytes 2359300
  1.8 0.7 %copy-start.4 = (f32[8,8]{1,0:T(8,128)S(1)}, f32[8,8]{1,0:T(8,128)}, u32[]{:S(2)}) copy-start(f32[8,8]{1,0:T(8,128)} %history_grad_ref.1) | copy-start | bytes 772
  2.5 0.7 %copy-start.7 = (s32[128,2]{0,1:T(2,128)S(1)}, s32[128,2]{0,1:T(2,128)}, u32[]{:S(2)}) copy-start(s32[128,2]{0,1:T(2,128)} %param.6) | copy-start | bytes 3076
  4.5 6.0 %collective-permute-start = (bf16[72,1536]{1,0:T(8,128)(2,1)S(1)}, bf16[72,1536]{1,0:T(8,128)(2,1)S(1)}, u32[]{:S(2)}, u32[]{:S(2)}) collective-permute-start(bf16[72,1536]{1,0:T(8,128)(2,1)S(1)} %get-tuple-element.20), channel_id=1, source_target_pairs={{0,1},{1,0},{2,3},{3,2},{4,5},{5,4},{6,7},{7,6},{8,9},{9,8},{10,11... | collective-permute-start | bytes 663560 | tf_op jit(solution)/shard_map/ppermute | solution.py:165
  5.0 17.9 %collective-permute-start.1 = (bf16[72,1536]{1,0:T(8,128)(2,1)S(1)}, bf16[72,1536]{1,0:T(8,128)(2,1)S(1)}, u32[]{:S(2)}, u32[]{:S(2)}) collective-permute-start(bf16[72,1536]{1,0:T(8,128)(2,1)S(1)} %get-tuple-element.21), channel_id=1, source_target_pairs={{0,2},{1,3},{2,0},{3,1},{4,6},{5,7},{6,4},{7,5},{8,10},{9,11},{10,... | collective-permute-start | bytes 663560 | tf_op jit(solution)/shard_map/ppermute | solution.py:165
  7.7 19.5 %collective-permute-start.2 = (bf16[72,1536]{1,0:T(8,128)(2,1)S(1)}, bf16[72,1536]{1,0:T(8,128)(2,1)S(1)}, u32[]{:S(2)}, u32[]{:S(2)}) collective-permute-start(bf16[72,1536]{1,0:T(8,128)(2,1)S(1)} %get-tuple-element.22), channel_id=1, source_target_pairs={{0,3},{1,2},{2,1},{3,0},{4,7},{5,6},{6,5},{7,4},{8,11},{9,10},{10,... | collective-permute-start | bytes 663560 | tf_op jit(solution)/shard_map/ppermute | solution.py:165
  7.7 28.1 %collective-permute-start.3 = (bf16[72,1536]{1,0:T(8,128)(2,1)S(1)}, bf16[72,1536]{1,0:T(8,128)(2,1)S(1)}, u32[]{:S(2)}, u32[]{:S(2)}) collective-permute-start(bf16[72,1536]{1,0:T(8,128)(2,1)S(1)} %get-tuple-element.25), channel_id=1, source_target_pairs={{0,4},{1,5},{2,6},{3,7},{4,0},{5,1},{6,2},{7,3},{8,12},{9,13},{10,... | collective-permute-start | bytes 663560 | tf_op jit(solution)/shard_map/ppermute | solution.py:165
  10.5 25.3 %collective-permute-start.4 = (bf16[72,1536]{1,0:T(8,128)(2,1)S(1)}, bf16[72,1536]{1,0:T(8,128)(2,1)S(1)}, u32[]{:S(2)}, u32[]{:S(2)}) collective-permute-start(bf16[72,1536]{1,0:T(8,128)(2,1)S(1)} %get-tuple-element.26), channel_id=1, source_target_pairs={{0,5},{1,4},{2,7},{3,6},{4,1},{5,0},{6,3},{7,2},{8,13},{9,12},{10,... | collective-permute-start | bytes 663560 | tf_op jit(solution)/shard_map/ppermute | solution.py:165
  10.5 25.3 %collective-permute-start.5 = (bf16[72,1536]{1,0:T(8,128)(2,1)S(1)}, bf16[72,1536]{1,0:T(8,128)(2,1)S(1)}, u32[]{:S(2)}, u32[]{:S(2)}) collective-permute-start(bf16[72,1536]{1,0:T(8,128)(2,1)S(1)} %get-tuple-element.27), channel_id=1, source_target_pairs={{0,6},{1,7},{2,4},{3,5},{4,2},{5,3},{6,0},{7,1},{8,14},{9,15},{10,... | collective-permute-start | bytes 663560 | tf_op jit(solution)/shard_map/ppermute | solution.py:165
  22.9 16.2 %collective-permute-start.6 = (bf16[72,1536]{1,0:T(8,128)(2,1)S(1)}, bf16[72,1536]{1,0:T(8,128)(2,1)S(1)}, u32[]{:S(2)}, u32[]{:S(2)}) collective-permute-start(bf16[72,1536]{1,0:T(8,128)(2,1)S(1)} %get-tuple-element.28), channel_id=1, source_target_pairs={{0,7},{1,6},{2,5},{3,4},{4,3},{5,2},{6,1},{7,0},{8,15},{9,14},{10,... | collective-permute-start | bytes 663560 | tf_op jit(solution)/shard_map/ppermute | solution.py:165
  27.2 2.8 %copy-start = (bf16[1,1024,3072]{2,1,0:T(8,128)(2,1)S(1)}, bf16[1,1024,3072]{2,1,0:T(8,128)(2,1)}, u32[]{:S(2)}) copy-start(bf16[1,1024,3072]{2,1,0:T(8,128)(2,1)} %param.7) | copy-start | bytes 18874372
  29.9 1.1 %copy-start.3 = (bf16[128,3072]{1,0:T(8,128)(2,1)S(1)}, bf16[128,3072]{1,0:T(8,128)(2,1)}, u32[]{:S(2)}) copy-start(bf16[128,3072]{1,0:T(8,128)(2,1)} %refs_8_.1) | copy-start | bytes 2359300
  31.1 0.7 %copy-start.5 = (f32[8,8]{1,0:T(8,128)S(1)}, f32[8,8]{1,0:T(8,128)}, u32[]{:S(2)}) copy-start(f32[8,8]{1,0:T(8,128)} %history_grad_ref.1) | copy-start | bytes 772
  31.8 0.7 %copy-start.6 = (f32[8,8]{1,0:T(8,128)S(1)}, f32[8,8]{1,0:T(8,128)}, u32[]{:S(2)}) copy-start(f32[8,8]{1,0:T(8,128)} %history_hidden_ref.1) | copy-start | bytes 772
  32.4 0.7 %copy-start.8 = (s32[128,2]{0,1:T(2,128)S(1)}, s32[128,2]{0,1:T(2,128)}, u32[]{:S(2)}) copy-start(s32[128,2]{0,1:T(2,128)} %param.6) | copy-start | bytes 3076
  33.1 6.0 %copy-start.1 = (bf16[1,1024,3072]{2,1,0:T(8,128)(2,1)S(1)}, bf16[1,1024,3072]{2,1,0:T(8,128)(2,1)}, u32[]{:S(2)}) copy-start(bf16[1,1024,3072]{2,1,0:T(8,128)(2,1)} %param.7) | copy-start | bytes 18874372
  42.2 22.1 %all-to-all-start = ((f32[32,1,128]{2,1,0:T(1,128)}), f32[32,1,128]{2,1,0:T(1,128)S(1)}, u32[]{:S(2)}, u32[]{:S(2)}) async-start(f32[32,1,128]{2,1,0:T(1,128)} %bitcast.4), calls=%async_computation | async-start | bytes 32768 | tf_op jit(solution)/shard_map/all_to_all | solution.py:196
  64.3 0.6 copy-start.9

commit v2 on v0

--- a/solution.py
+++ b/solution.py
@@ -1,10 +1,241 @@
+import functools
+
 import jax
 import jax.numpy as jnp
 from jax import lax
+from jax.experimental import pallas as pl
+from jax.experimental.pallas import tpu as pltpu
 from jax.sharding import PartitionSpec as P
 
 
-def per_device(grad_out, expert_ids, down_weight, history_grad, history_hidden):
+VMEM = pl.BlockSpec(memory_space=pltpu.VMEM)
+ANY = pl.BlockSpec(memory_space=pl.ANY)
+
+
+def choice_map(ids, order):
+    return (ids[0:1, :] == order) | (ids[1:2, :] == order)
+
+
+def pick(values, index):
+    lanes = lax.broadcasted_iota(jnp.int32, values.shape, 1)
+    return jnp.sum(jnp.where(lanes == index, values, 0.0), axis=1, keepdims=True)
+
+
+def dispatch_kernel(experts, capacity, first, *refs):
+    ids_hbm, grad_hbm, history_hbm = refs[:3]
+    ids_ref, grad_ref, history_ref, sems = refs[-4:]
+    out_refs = refs[-4 - experts // 2 : -4]
+    copies = [
+        pltpu.make_async_copy(source, target, sems.at[i])
+        for i, (source, target) in enumerate(
+            ((ids_hbm, ids_ref), (history_hbm, history_ref), (grad_hbm, grad_ref))
+        )
+    ]
+    for copy in copies:
+        copy.start()
+    tokens, features = grad_ref.shape
+    half = features // 2
+    base = capacity // 8 * 8
+    rest = capacity - base
+    me = lax.axis_index("expert")
+    order = lax.broadcasted_iota(jnp.int32, (experts, tokens), 0) ^ me
+    before = (
+        lax.broadcasted_iota(jnp.int32, (tokens, tokens), 0)
+        < lax.broadcasted_iota(jnp.int32, (tokens, tokens), 1)
+    )
+    rows = lax.broadcasted_iota(jnp.int32, (2 * capacity, tokens), 0)
+    low_slot = jnp.where(rows < capacity, rows, -1)
+    high_slot = jnp.where(
+        rows < capacity, -1, jnp.where(rows < capacity + rest, rows - capacity + base, rows - capacity - rest)
+    )
+    copies[0].wait()
+    named = choice_map(ids_ref[...], order)
+    slot = jnp.dot(
+        jnp.where(named, 1.0, 0.0).astype(jnp.bfloat16),
+        jnp.where(before, 1.0, 0.0).astype(jnp.bfloat16),
+        preferred_element_type=jnp.float32,
+    ).astype(jnp.int32)
+    slot = jnp.where(named, slot, -2)
+    copies[1].wait()
+    scale = 1.0 / jnp.max(history_ref[...], axis=0, keepdims=True)
+    copies[2].wait()
+    stacked = jnp.concatenate([grad_ref[:, :half], grad_ref[:, half:]], axis=0)
+    for i, out_ref in enumerate(out_refs):
+        k = first + i
+        mine = slot[k : k + 1, :]
+        low = jnp.where(mine == low_slot, 1.0, 0.0)
+        high = jnp.where(mine == high_slot, 1.0, 0.0)
+        select = jnp.concatenate([low, high], axis=1).astype(jnp.bfloat16)
+        rowsum = jnp.dot(select, stacked, preferred_element_type=jnp.float32)
+        factor = pick(scale, me ^ k)
+        out_ref[...] = jnp.clip(rowsum * factor, -1.0, 1.0).astype(jnp.bfloat16)
+
+
+def gather_rows(blocks, capacity, rows_ref):
+    base = capacity // 8 * 8
+    rest = capacity - base
+    half = rows_ref.shape[1] // 2
+    step = base + 8
+    keep = lax.broadcasted_iota(jnp.int32, (8, half), 0) < rest
+    for i, block in enumerate(blocks):
+        at = i * step
+        rows_ref[at : at + base, :half] = block[0:base, :]
+        rows_ref[at : at + base, half:] = block[base + 8 :, :]
+        mixed = block[base : base + 8, :].astype(jnp.float32)
+        turned = jnp.concatenate([mixed[rest:], mixed[:rest]], axis=0)
+        rows_ref[at + base : at + step, :half] = jnp.where(keep, mixed, 0.0).astype(jnp.bfloat16)
+        rows_ref[at + base : at + step, half:] = jnp.where(keep, turned, 0.0).astype(jnp.bfloat16)
+
+
+def largest(product, restore):
+    peak = jnp.max(jnp.abs(product), axis=0, keepdims=True)
+    return jnp.max(peak, axis=1, keepdims=True) * restore
+
+
+def prepare_kernel(experts, weight_ref, ids_ref, grad_ref, turned_ref, vector_ref):
+    turned_ref[...] = weight_ref[...].T
+    tokens = grad_ref.shape[0]
+    order = lax.broadcasted_iota(jnp.int32, (experts, tokens), 0)
+    named = choice_map(ids_ref[...], order)
+    row_peak = jnp.max(jnp.abs(grad_ref[...].astype(jnp.float32)), axis=1, keepdims=True)
+    row_peak = jnp.broadcast_to(row_peak, (tokens, tokens)).T[0:1, :]
+    grad_peak = jnp.max(jnp.where(named, row_peak, 0.0), axis=1, keepdims=True)
+    lanes = lax.broadcasted_iota(jnp.int32, (experts, 128), 1)
+    spread = jnp.where(
+        lanes == lax.broadcasted_iota(jnp.int32, (experts, 128), 0), grad_peak, 0.0
+    )
+    vector_ref[...] = jnp.max(spread, axis=0, keepdims=True)
+
+
+def project_kernel(experts, capacity, count, *refs):
+    blocks = refs[:count]
+    turned_ref, history_grad_ref, vector_ref, product_ref, peaks_ref, rows_ref = refs[count:]
+    me = lax.axis_index("expert")
+    gather_rows(blocks, capacity, rows_ref)
+    product = jnp.dot(rows_ref[...], turned_ref[...], preferred_element_type=jnp.float32)
+    product_ref[...] = product
+    scale_in = pick(1.0 / jnp.max(history_grad_ref[...], axis=0, keepdims=True), me)
+    peak = largest(product, 1.0 / scale_in)
+    lane = lax.broadcasted_iota(jnp.int32, (1, 128), 1)
+    vector = jnp.maximum(vector_ref[...], jnp.where(lane == experts + me, peak, 0.0))
+    peaks_ref[...] = jnp.broadcast_to(vector, peaks_ref.shape)
+
+
+def assemble_kernel(capacity, early_ref, late_ref, history_grad_ref, history_hidden_ref, out_ref):
+    me = lax.axis_index("expert")
+    chip = me // 2
+    first_core = (me & 1) == 0
+    step = capacity // 8 * 8 + 8
+    scale_in = pick(1.0 / jnp.max(history_grad_ref[...], axis=0, keepdims=True), me)
+    scale_hidden = pick(1.0 / jnp.max(history_hidden_ref[...], axis=0, keepdims=True), me)
+    restore = 1.0 / scale_in
+    pairs = early_ref.shape[0] // step // 2
+    for j in range(2 * pairs):
+        ref, at = (early_ref, j) if j < pairs else (late_ref, j - pairs)
+        at = 2 * at * step
+        a, b = ref[at : at + capacity, :], ref[at + step : at + step + capacity, :]
+        both = jnp.concatenate([jnp.where(first_core, a, b), jnp.where(first_core, b, a)], axis=0)
+        both = jnp.clip(both * restore * scale_hidden, -1.0, 1.0).astype(jnp.bfloat16)
+        start = pl.multiple_of((chip ^ j) * 2 * capacity, 8)
+        out_ref[pl.ds(start, 2 * capacity), :] = both
+
+
+def sending_order(experts):
+    half = experts // 2
+    return [
+        *range(half, half + half // 2), *range(2, half), 1, *range(half + half // 2, experts)
+    ]
+
+
+def fast_device(grad_out, expert_ids, down_weight, history_grad, history_hidden):
+    tokens, features = grad_out.shape
+    experts = history_grad.shape[1]
+    capacity = tokens * 9 // 32
+    units = down_weight.shape[1]
+    half = experts // 2
+    devices = lax.axis_size("dp") * lax.axis_size("expert")
+    ids = expert_ids.T
+    weight = down_weight[0]
+    bf16, f32 = jnp.bfloat16, jnp.float32
+    block = jax.ShapeDtypeStruct((2 * capacity, features // 2), bf16)
+
+    def dispatch(first, after):
+        return pl.pallas_call(
+            functools.partial(dispatch_kernel, experts, capacity, first),
+            out_shape=[block] * half,
+            in_specs=[pl.BlockSpec(memory_space=pltpu.HBM)] * 3 + [ANY] * len(after),
+            out_specs=[VMEM] * half,
+            scratch_shapes=[
+                pltpu.VMEM(ids.shape, jnp.int32),
+                pltpu.VMEM(grad_out.shape, bf16),
+                pltpu.VMEM(history_grad.shape, f32),
+                pltpu.SemaphoreType.DMA((3,)),
+            ],
+            compiler_params=pltpu.CompilerParams(vmem_limit_bytes=16 << 20),
+            cost_estimate=pl.CostEstimate(
+                flops=1 << 28, bytes_accessed=grad_out.size * 4, transcendentals=0
+            ),
+        )(*(pltpu.with_memory_space_constraint(x, pltpu.HBM) for x in (ids, grad_out, history_grad)), *after)
+
+    far = dispatch(half, ())
+    near = dispatch(0, (far[0],))
+    received = [near[0]] + [None] * (experts - 1)
+    for k in sending_order(experts):
+        received[k] = lax.ppermute((near + far)[k], "expert", [(i, i ^ k) for i in range(experts)])
+    rows = half * (capacity // 8 * 8 + 8)
+    product = jax.ShapeDtypeStruct((rows, units), f32)
+    scratch = [pltpu.VMEM((rows, features), bf16)]
+    params = pltpu.CompilerParams(vmem_limit_bytes=24 << 20)
+    cost = pl.CostEstimate(
+        flops=rows * units * features * 2, bytes_accessed=units * features * 2, transcendentals=0
+    )
+    turned, vector = pl.pallas_call(
+        functools.partial(prepare_kernel, experts),
+        out_shape=[
+            jax.ShapeDtypeStruct((features, units), bf16),
+            jax.ShapeDtypeStruct((1, 128), f32),
+        ],
+        in_specs=[VMEM] * 3,
+        out_specs=[VMEM] * 2,
+        compiler_params=params,
+        cost_estimate=cost,
+        name="prepare",
+    )(weight, ids, grad_out)
+
+    def project(blocks, vector, copies):
+        return pl.pallas_call(
+            functools.partial(project_kernel, experts, capacity, len(blocks)),
+            out_shape=[product, jax.ShapeDtypeStruct((copies, 128), f32)],
+            in_specs=[VMEM] * (len(blocks) + 3),
+            out_specs=[VMEM] * 2,
+            scratch_shapes=scratch,
+            compiler_params=params,
+            cost_estimate=cost,
+        )(*blocks, turned, history_grad, vector)
+
+    early, vector = project(received[:half], vector, 1)
+    late, peaks = project(received[half:], vector, devices)
+    everyone = lax.all_to_all(peaks, ("dp", "expert"), 0, 0, tiled=True)
+    hidden = pl.pallas_call(
+        functools.partial(assemble_kernel, capacity),
+        out_shape=jax.ShapeDtypeStruct((experts * capacity, units), bf16),
+        in_specs=[VMEM] * 4,
+        out_specs=VMEM,
+        compiler_params=pltpu.CompilerParams(vmem_limit_bytes=8 << 20),
+        cost_estimate=pl.CostEstimate(
+            flops=1 << 22, bytes_accessed=experts * capacity * units * 4, transcendentals=0
+        ),
+        name="assemble",
+    )(early, late, history_grad, history_hidden)
+    top = jnp.max(everyone, axis=0)
+    new_history_grad = jnp.concatenate([history_grad[1:], top[None, :experts]], axis=0)
+    new_history_hidden = jnp.concatenate(
+        [history_hidden[1:], top[None, experts : 2 * experts]], axis=0
+    )
+    return hidden.reshape(1, 1, -1, units), new_history_grad, new_history_hidden
+
+
+def general_device(grad_out, expert_ids, down_weight, history_grad, history_hidden):
     tok_rows = grad_out.shape[0]
     experts = history_grad.shape[1]
     slices = lax.axis_size("expert") // experts
@@ -49,6 +280,19 @@
     return (hidden_scaled, new_history_grad, new_history_hidden)
 
 
+def is_fast(expert_devices, experts, capacity):
+    power = experts & (experts - 1) == 0 and experts >= 4
+    return expert_devices == experts and power and capacity % 8 == 4
+
+
+def per_device(grad_out, expert_ids, down_weight, history_grad, history_hidden):
+    experts = history_grad.shape[1]
+    capacity = grad_out.shape[0] * 9 // 32
+    fast = is_fast(lax.axis_size("expert"), experts, capacity)
+    device = fast_device if fast else general_device
+    return device(grad_out, expert_ids, down_weight, history_grad, history_hidden)
+
+
 def solution(mesh):
     in_specs = (
         P(("dp", "expert"), None),

time: 113 us -> 64.1 us (0.57)
  blocking collectives: 37.8 us -> 0 us
  waiting for transfers between devices: 45.2 us -> 21.4 us
  starting transfers between devices: 6.49 us -> 24.9 us
  Pallas kernels: 0 us -> 11.4 us
  matrix products: 8.85 us -> 0 us
  other arithmetic: 8.16 us -> 0.66 us
    all_to_all x1, waiting for transfers between devices: 45.2 us -> 5.98 us  [fast_device(): everyone = lax.all_to_all(peaks, ('dp', 'expert'), 0, 0, tiled=True)]
    pmax x1 -> x0, blocking collectives: 37.8 us -> none  [per_device(): grad_amax, hidden_amax = lax.pmax((grad_peak, hidden_vec), ('dp', 'expert'))]
    ppermute x0 -> x7, waiting for transfers between devices: none -> 15.4 us  [fast_device(): lax.ppermute((near + far)[k], 'expert', [(i, i ^ k) for i in range(expert...]
    pallas_call x0 -> x6, Pallas kernels: none -> 11.4 us  [the longest x2 3.74 us: dispatch(): pl.pallas_call(functools.partial(dispatch_kernel, experts, capacity, firs...]
    ppermute x0 -> x7, starting transfers between devices: none -> 10 us  [fast_device(): lax.ppermute((near + far)[k], 'expert', [(i, i ^ k) for i in range(expert...]
    dot_general x2 -> x0, matrix products: 8.85 us -> none  [the longest x1 7.11 us: per_device(): jnp.einsum('sic,uc->siu', received, weight_block, preferred_element_type=...]
    all_to_all x1, starting transfers between devices: 6.49 us -> 14.9 us  [fast_device(): everyone = lax.all_to_all(peaks, ('dp', 'expert'), 0, 0, tiled=True)]
    convert_element_type x2 -> x0, other arithmetic: 3.85 us -> none  [the longest x1 3.85 us: per_device(): quantized = jnp.clip(gathered.reshape(experts, capacity, -1) * scale_in[:...]
  transfers between devices with their start and end apart: 1 -> 8, of which waited for: 1 -> 4; matrix products, arithmetic and copies ran while one was open for 1% -> 0% of each run, Pallas kernels for 0% -> 9%
where the time goes in v2:
time: 64.1 us; the launch traced here: 63.8 us
  starting transfers between devices  24.9 us (39%)
  waiting for transfers between devices  21.4 us (33%)
  Pallas kernels  11.4 us (18%)
  local copies, waits for them, and re-layouts  4.69 us (7%)
  between operations  0.73 us (1%)
  other arithmetic  0.66 us (1%)
    ppermute x7, waiting for transfers between devices, fast_device(): lax.ppermute((near + far)[k], 'expert', [(i, i ^ k) for i in range(expert...  15.4 us
    all_to_all x1, starting transfers between devices, fast_device(): everyone = lax.all_to_all(peaks, ('dp', 'expert'), 0, 0, tiled=True)  14.9 us
    ppermute x7, starting transfers between devices, fast_device(): lax.ppermute((near + far)[k], 'expert', [(i, i ^ k) for i in range(expert...  10 us
    all_to_all x1, waiting for transfers between devices, fast_device(): everyone = lax.all_to_all(peaks, ('dp', 'expert'), 0, 0, tiled=True)  5.98 us
    unnamed x10, local copies, waits for them, and re-layouts  4.61 us
    pallas_call x2, Pallas kernels, dispatch(): pl.pallas_call(functools.partial(dispatch_kernel, experts, capacity, firs...  3.74 us
    pallas_call x1, Pallas kernels, fast_device(): pl.pallas_call(functools.partial(prepare_kernel, experts), out_shape=[jax...  3.3 us
    pallas_call x2, Pallas kernels, project(): pl.pallas_call(functools.partial(project_kernel, experts, capacity, len(b...  3.18 us
  transfers between devices with their start and end apart: 8, of which 4 were waited for; matrix products, arithmetic and copies ran while one was open for 0% of the time, Pallas kernels for 9%

profile of v2, /device:TPU:0, one launch (start us, length us, event | category | flops | bytes accessed | tf_op | source)
XLA Modules:
  0.0 63.8 jit_solution(15979074321519059390)
XLA Ops:
  0.6 0.0 copy-start.2
  0.6 1.9 %shard_map.76 = (bf16[72,1536]{1,0:T(8,128)(2,1)S(1)}, bf16[72,1536]{1,0:T(8,128)(2,1)S(1)}, bf16[72,1536]{1,0:T(8,128)(2,1)S(1)}, bf16[72,1536]{1,0:T(8,128)(2,1)S(1)}) custom-call(s32[2,128]{1,0:T(2,128)} %bitcast.11, bf16[128,3072]{1,0:T(8,128)(2,1)} %grad_ref.1, f32[8,8]{1,0:T(8,128)} %history_grad_ref.1), custom_call_target="tpu_custom_call" | custom-call | flops 268435456 | bytes 1572864 | tf_op jit(solution)/shard_map/pallas_call | solution.py:163
  2.5 1.9 %shard_map.77 = (bf16[72,1536]{1,0:T(8,128)(2,1)S(1)}, bf16[72,1536]{1,0:T(8,128)(2,1)S(1)}, bf16[72,1536]{1,0:T(8,128)(2,1)S(1)}, bf16[72,1536]{1,0:T(8,128)(2,1)S(1)}) custom-call(s32[2,128]{1,0:T(2,128)} %bitcast.12, bf16[128,3072]{1,0:T(8,128)(2,1)} %grad_ref.1, f32[8,8]{1,0:T(8,128)} %history_grad_ref.1, bf16[72,1536]{1,0:T(8,128)(2,1)S(1)} %get-tuple-element.17.refs_3_), custom_call_target="tpu_custom_call" | custom-call | flops 268435456 | bytes 1572864 | tf_op jit(solution)/shard_map/pallas_call | solution.py:163
  4.4 0.6 collective-permute-start
  5.0 2.6 %collective-permute-start.1 = (bf16[72,1536]{1,0:T(8,128)(2,1)S(1)}, bf16[72,1536]{1,0:T(8,128)(2,1)S(1)}, u32[]{:S(2)}, u32[]{:S(2)}) collective-permute-start(bf16[72,1536]{1,0:T(8,128)(2,1)S(1)} %get-tuple-element.20), channel_id=1, source_target_pairs={{0,2},{1,3},{2,0},{3,1},{4,6},{5,7},{6,4},{7,5},{8,10},{9,11},{10,... | collective-permute-start | bytes 663560 | tf_op jit(solution)/shard_map/ppermute | solution.py:184
  7.6 0.0 collective-permute-start.2
  7.6 2.8 %collective-permute-start.3 = (bf16[72,1536]{1,0:T(8,128)(2,1)S(1)}, bf16[72,1536]{1,0:T(8,128)(2,1)S(1)}, u32[]{:S(2)}, u32[]{:S(2)}) collective-permute-start(bf16[72,1536]{1,0:T(8,128)(2,1)S(1)} %get-tuple-element.17.refs_3_), channel_id=1, source_target_pairs={{0,4},{1,5},{2,6},{3,7},{4,0},{5,1},{6,2},{7,3},{8,12},{9,13},{10,... | collective-permute-start | bytes 663560 | tf_op jit(solution)/shard_map/ppermute | solution.py:184
  10.4 3.6 %collective-permute-start.5 = (bf16[72,1536]{1,0:T(8,128)(2,1)S(1)}, bf16[72,1536]{1,0:T(8,128)(2,1)S(1)}, u32[]{:S(2)}, u32[]{:S(2)}) collective-permute-start(bf16[72,1536]{1,0:T(8,128)(2,1)S(1)} %get-tuple-element.26), channel_id=1, source_target_pairs={{0,6},{1,7},{2,4},{3,5},{4,2},{5,3},{6,0},{7,1},{8,14},{9,15},{10,... | collective-permute-start | bytes 663560 | tf_op jit(solution)/shard_map/ppermute | solution.py:184
  14.0 8.8 %collective-permute-done.1.refs_2_ = bf16[72,1536]{1,0:T(8,128)(2,1)S(1)} collective-permute-done((bf16[72,1536]{1,0:T(8,128)(2,1)S(1)}, bf16[72,1536]{1,0:T(8,128)(2,1)S(1)}, u32[]{:S(2)}, u32[]{:S(2)}) %collective-permute-start.1) | collective-permute-done | bytes 221216 | tf_op jit(solution)/shard_map/ppermute | solution.py:184
  22.9 0.4 collective-permute-start.6
  23.3 2.8 %copy-done = bf16[1,1024,3072]{2,1,0:T(8,128)(2,1)S(1)} copy-done((bf16[1,1024,3072]{2,1,0:T(8,128)(2,1)S(1)}, bf16[1,1024,3072]{2,1,0:T(8,128)(2,1)}, u32[]{:S(2)}) %copy-start) | copy-done | bytes 6291480
  26.0 1.1 %copy-done.1 = bf16[128,3072]{1,0:T(8,128)(2,1)S(1)} copy-done((bf16[128,3072]{1,0:T(8,128)(2,1)S(1)}, bf16[128,3072]{1,0:T(8,128)(2,1)}, u32[]{:S(2)}) %copy-start.1) | copy-done | bytes 786456
  27.2 0.7 %copy-done.4 = s32[128,2]{0,1:T(2,128)S(1)} copy-done((s32[128,2]{0,1:T(2,128)S(1)}, s32[128,2]{0,1:T(2,128)}, u32[]{:S(2)}) %copy-start.4) | copy-done | bytes 1048
  27.9 3.3 %prepare.1 = (bf16[3072,1024]{1,0:T(8,128)(2,1)S(1)}, f32[1,128]{1,0:T(1,128)S(1)}) custom-call(bf16[1024,3072]{1,0:T(8,128)(2,1)S(1)} %bitcast.10, s32[2,128]{1,0:T(2,128)S(1)} %bitcast.13, bf16[128,3072]{1,0:T(8,128)(2,1)S(1)} %copy-done.1), custom_call_target="tpu_custom_call" | custom-call | flops 1006632960 | bytes 6291456 | tf_op jit(solution)/shard_map/prepare/pallas_call | solution.py:192
  31.2 1.3 %shard_map.78 = (f32[160,1024]{1,0:T(8,128)S(1)}, f32[1,128]{1,0:T(1,128)S(1)}) custom-call(bf16[72,1536]{1,0:T(8,128)(2,1)S(1)} %get-tuple-element.18.refs_0_, bf16[72,1536]{1,0:T(8,128)(2,1)S(1)} %collective-permute-done.refs_1_, bf16[72,1536]{1,0:T(8,128)(2,1)S(1)} %collective-permute-done.1.refs_2_, bf16[72,1536]{1,0:T(8,128)(2,1)S(1)} %collective-permute-done.2.refs_3_, ...), custom_call_target="tpu_custom_call" | custom-call | flops 1006632960 | bytes 6291456 | tf_op jit(solution)/shard_map/pallas_call | solution.py:206
  32.5 2.9 %collective-permute-done.5.refs_2_ = bf16[72,1536]{1,0:T(8,128)(2,1)S(1)} collective-permute-done((bf16[72,1536]{1,0:T(8,128)(2,1)S(1)}, bf16[72,1536]{1,0:T(8,128)(2,1)S(1)}, u32[]{:S(2)}, u32[]{:S(2)}) %collective-permute-start.5) | collective-permute-done | bytes 221216 | tf_op jit(solution)/shard_map/ppermute | solution.py:184
  35.4 3.7 %collective-permute-done.6.refs_3_ = bf16[72,1536]{1,0:T(8,128)(2,1)S(1)} collective-permute-done((bf16[72,1536]{1,0:T(8,128)(2,1)S(1)}, bf16[72,1536]{1,0:T(8,128)(2,1)S(1)}, u32[]{:S(2)}, u32[]{:S(2)}) %collective-permute-start.6) | collective-permute-done | bytes 221216 | tf_op jit(solution)/shard_map/ppermute | solution.py:184
  39.1 1.9 %shard_map.79 = (f32[160,1024]{1,0:T(8,128)S(1)}, f32[32,128]{1,0:T(8,128)}) custom-call(bf16[72,1536]{1,0:T(8,128)(2,1)S(1)} %collective-permute-done.3.refs_0_, bf16[72,1536]{1,0:T(8,128)(2,1)S(1)} %collective-permute-done.4.refs_1_, bf16[72,1536]{1,0:T(8,128)(2,1)S(1)} %collective-permute-done.5.refs_2_, ...), custom_call_target="tpu_custom_call" | custom-call | flops 1006632960 | bytes 6291456 | tf_op jit(solution)/shard_map/pallas_call | solution.py:206
  41.0 14.9 %all-to-all-start = ((f32[32,1,128]{2,1,0:T(1,128)}), f32[32,1,128]{2,1,0:T(1,128)S(1)}, u32[]{:S(2)}, u32[]{:S(2)}) async-start(f32[32,1,128]{2,1,0:T(1,128)} %bitcast.4), calls=%async_computation | async-start | bytes 32768 | tf_op jit(solution)/shard_map/all_to_all | solution.py:218
  55.9 1.1 %assemble.1 = bf16[288,1024]{1,0:T(8,128)(2,1)} custom-call(f32[160,1024]{1,0:T(8,128)S(1)} %get-tuple-element.24.early_ref, f32[160,1024]{1,0:T(8,128)S(1)} %get-tuple-element.29.late_ref, f32[8,8]{1,0:T(8,128)S(1)} %copy-done.2, f32[8,8]{1,0:T(8,128)S(1)} %copy-done.3), custom_call_target="tpu_custom_call" | custom-call | flops 4194304 | bytes 1179648 | tf_op jit(solution)/shard_map/assemble/pallas_call | solution.py:219
  57.1 6.0 %all-to-all-done = f32[32,1,128]{2,1,0:T(1,128)S(1)} async-done(((f32[32,1,128]{2,1,0:T(1,128)}), f32[32,1,128]{2,1,0:T(1,128)S(1)}, u32[]{:S(2)}, u32[]{:S(2)}) %all-to-all-start) | async-done | bytes 16416 | tf_op jit(solution)/shard_map/all_to_all | solution.py:218
  63.1 0.1 reduce_max.9
  63.1 0.1 slice_bitcast_fusion
  63.2 0.6 pad_maximum_fusion
  (13 shorter events, 0.0 us)
Async XLA Ops:
  0.6 30.6 %copy-start.2 = (f32[8,8]{1,0:T(8,128)S(1)}, f32[8,8]{1,0:T(8,128)}, u32[]{:S(2)}) copy-start(f32[8,8]{1,0:T(8,128)} %history_grad_ref.1) | copy-start | bytes 772
  4.4 6.0 %collective-permute-start = (bf16[72,1536]{1,0:T(8,128)(2,1)S(1)}, bf16[72,1536]{1,0:T(8,128)(2,1)S(1)}, u32[]{:S(2)}, u32[]{:S(2)}) collective-permute-start(bf16[72,1536]{1,0:T(8,128)(2,1)S(1)} %get-tuple-element.19), channel_id=1, source_target_pairs={{0,1},{1,0},{2,3},{3,2},{4,5},{5,4},{6,7},{7,6},{8,9},{9,8},{10,11... | collective-permute-start | bytes 663560 | tf_op jit(solution)/shard_map/ppermute | solution.py:184
  5.0 17.9 %collective-permute-start.1 = (bf16[72,1536]{1,0:T(8,128)(2,1)S(1)}, bf16[72,1536]{1,0:T(8,128)(2,1)S(1)}, u32[]{:S(2)}, u32[]{:S(2)}) collective-permute-start(bf16[72,1536]{1,0:T(8,128)(2,1)S(1)} %get-tuple-element.20), channel_id=1, source_target_pairs={{0,2},{1,3},{2,0},{3,1},{4,6},{5,7},{6,4},{7,5},{8,10},{9,11},{10,... | collective-permute-start | bytes 663560 | tf_op jit(solution)/shard_map/ppermute | solution.py:184
  7.6 23.6 %collective-permute-start.2 = (bf16[72,1536]{1,0:T(8,128)(2,1)S(1)}, bf16[72,1536]{1,0:T(8,128)(2,1)S(1)}, u32[]{:S(2)}, u32[]{:S(2)}) collective-permute-start(bf16[72,1536]{1,0:T(8,128)(2,1)S(1)} %get-tuple-element.21), channel_id=1, source_target_pairs={{0,3},{1,2},{2,1},{3,0},{4,7},{5,6},{6,5},{7,4},{8,11},{9,10},{10,... | collective-permute-start | bytes 663560 | tf_op jit(solution)/shard_map/ppermute | solution.py:184
  7.6 24.9 %collective-permute-start.3 = (bf16[72,1536]{1,0:T(8,128)(2,1)S(1)}, bf16[72,1536]{1,0:T(8,128)(2,1)S(1)}, u32[]{:S(2)}, u32[]{:S(2)}) collective-permute-start(bf16[72,1536]{1,0:T(8,128)(2,1)S(1)} %get-tuple-element.17.refs_3_), channel_id=1, source_target_pairs={{0,4},{1,5},{2,6},{3,7},{4,0},{5,1},{6,2},{7,3},{8,12},{9,13},{10,... | collective-permute-start | bytes 663560 | tf_op jit(solution)/shard_map/ppermute | solution.py:184
  10.4 22.1 %collective-permute-start.4 = (bf16[72,1536]{1,0:T(8,128)(2,1)S(1)}, bf16[72,1536]{1,0:T(8,128)(2,1)S(1)}, u32[]{:S(2)}, u32[]{:S(2)}) collective-permute-start(bf16[72,1536]{1,0:T(8,128)(2,1)S(1)} %get-tuple-element.25), channel_id=1, source_target_pairs={{0,5},{1,4},{2,7},{3,6},{4,1},{5,0},{6,3},{7,2},{8,13},{9,12},{10,... | collective-permute-start | bytes 663560 | tf_op jit(solution)/shard_map/ppermute | solution.py:184
  10.4 25.0 %collective-permute-start.5 = (bf16[72,1536]{1,0:T(8,128)(2,1)S(1)}, bf16[72,1536]{1,0:T(8,128)(2,1)S(1)}, u32[]{:S(2)}, u32[]{:S(2)}) collective-permute-start(bf16[72,1536]{1,0:T(8,128)(2,1)S(1)} %get-tuple-element.26), channel_id=1, source_target_pairs={{0,6},{1,7},{2,4},{3,5},{4,2},{5,3},{6,0},{7,1},{8,14},{9,15},{10,... | collective-permute-start | bytes 663560 | tf_op jit(solution)/shard_map/ppermute | solution.py:184
  22.9 16.2 %collective-permute-start.6 = (bf16[72,1536]{1,0:T(8,128)(2,1)S(1)}, bf16[72,1536]{1,0:T(8,128)(2,1)S(1)}, u32[]{:S(2)}, u32[]{:S(2)}) collective-permute-start(bf16[72,1536]{1,0:T(8,128)(2,1)S(1)} %get-tuple-element.27), channel_id=1, source_target_pairs={{0,7},{1,6},{2,5},{3,4},{4,3},{5,2},{6,1},{7,0},{8,15},{9,14},{10,... | collective-permute-start | bytes 663560 | tf_op jit(solution)/shard_map/ppermute | solution.py:184
  23.3 2.8 %copy-start = (bf16[1,1024,3072]{2,1,0:T(8,128)(2,1)S(1)}, bf16[1,1024,3072]{2,1,0:T(8,128)(2,1)}, u32[]{:S(2)}) copy-start(bf16[1,1024,3072]{2,1,0:T(8,128)(2,1)} %param.7) | copy-start | bytes 18874372
  26.0 1.1 %copy-start.1 = (bf16[128,3072]{1,0:T(8,128)(2,1)S(1)}, bf16[128,3072]{1,0:T(8,128)(2,1)}, u32[]{:S(2)}) copy-start(bf16[128,3072]{1,0:T(8,128)(2,1)} %grad_ref.1) | copy-start | bytes 2359300
  27.2 0.7 %copy-start.4 = (s32[128,2]{0,1:T(2,128)S(1)}, s32[128,2]{0,1:T(2,128)}, u32[]{:S(2)}) copy-start(s32[128,2]{0,1:T(2,128)} %param.6) | copy-start | bytes 3076
  31.2 24.7 %copy-start.3 = (f32[8,8]{1,0:T(8,128)S(1)}, f32[8,8]{1,0:T(8,128)}, u32[]{:S(2)}) copy-start(f32[8,8]{1,0:T(8,128)} %history_hidden_ref.1) | copy-start | bytes 772
  41.0 22.1 %all-to-all-start = ((f32[32,1,128]{2,1,0:T(1,128)}), f32[32,1,128]{2,1,0:T(1,128)S(1)}, u32[]{:S(2)}, u32[]{:S(2)}) async-start(f32[32,1,128]{2,1,0:T(1,128)} %bitcast.4), calls=%async_computation | async-start | bytes 32768 | tf_op jit(solution)/shard_map/all_to_all | solution.py:218
